TPU v7x, 256 devices: a whole 4x4x8 slice. The times are simulated.
256 devices in a mesh: img: 16 (over y, x), row: 16 (over z, core).
Axes of the slice: x: 4, y: 4, z: 8, core: 2. Of those that a mesh axis runs over, the one named last changes fastest.
Arguments:
- latent: bfloat16 [1024, 128, 512], P(('img', 'row')), parts along dimension 0, may hold values from -8 to 8
- attn_gain: float32 [512], replicated, may hold values from 0.5 to 1.5
- attn_shift: float32 [512], replicated, may hold values from -3 to 3
- w_query: bfloat16 [512, 512], replicated, may hold values from -2 to 2
- w_key: bfloat16 [512, 512], replicated, may hold values from -2 to 2
- w_value: bfloat16 [512, 512], replicated, may hold values from -0.25 to 0.25
- w_out: bfloat16 [512, 512], replicated, may hold values from -0.25 to 0.25
- conv_gain: float32 [512], replicated, may hold values from 0.5 to 1.5
- conv_shift: float32 [512], replicated, may hold values from -3 to 3
- w_conv: bfloat16 [3, 3, 512, 512], replicated, may hold values from -0.09375 to 0.09375
- conv_bias: float32 [512], replicated, may hold values from -3 to 3
Outputs:
- encoded: bfloat16 [1024, 128, 512], P(('img', 'row')), parts along dimension 0
There are 16 independent parts, one for each index of `img`. A program takes and returns all parts, laid end to end along the dimension named above; an argument that names none is the same for every part. Nothing has to cross between parts.
All inputs are finite; a program needn't handle non-finite values.
Results may differ from a plain program's by a relative error of at most 0.011.
Values may be sent and summed in bfloat16 or wider, within the bound.
A program may use at most 128 MiB of HBM per device.

v0:
```python
import jax
import jax.numpy as jnp
from jax import lax
from jax.sharding import PartitionSpec as P

C = 512
GROUPS = 32
W = 128


epsilon = 1e-06


def copy_for_each(shard, axis):
    copies = jnp.broadcast_to(shard, (lax.axis_size(axis), *shard.shape))
    return lax.all_to_all(copies, axis, split_axis=0, concat_axis=0, tiled=True)


def taken_together(shard, axis):
    return copy_for_each(shard, axis).sum(axis=0)


def together(arrays, axis):
    line, at, done = (jnp.concatenate([a.reshape(-1) for a in arrays]), 0, [])
    total = taken_together(line, axis)
    for a in arrays:
        done.append(total[at : at + a.size].reshape(a.shape))
        at += a.size
    return tuple(done)


def with_halo(cells, sides, width):
    for axis, dim in sides:
        count = lax.axis_size(axis)
        ends = count - 1
        head = lax.slice_in_dim(cells, 0, width, axis=dim)
        tail = lax.slice_in_dim(cells, cells.shape[dim] - width, cells.shape[dim], axis=dim)
        cells = jnp.concatenate(
            [
                lax.ppermute(tail, axis, [(i, (i + 1) % count) for i in range(ends)]),
                cells,
                lax.ppermute(head, axis, [((i + 1) % count, i) for i in range(ends)]),
            ],
            axis=dim,
        )
    return cells


def group_stats(grouped, count):
    first, second = together(
        (jnp.sum(grouped, axis=(0, 2)), jnp.sum(grouped * grouped, axis=(0, 2))), "row"
    )
    centre = first / count
    spread = second / count - centre * centre
    return (centre, spread)


def group_norm(field, gain, shift):
    grouped = field.reshape(field.shape[0], GROUPS, C // GROUPS)
    count = field.shape[0] * lax.axis_size("row") * (C // GROUPS)
    centre, spread = group_stats(grouped, count)
    normed = (grouped - centre[None, :, None]) * lax.rsqrt(spread + epsilon)[None, :, None]
    return normed.reshape(field.shape) * gain + shift


def attend(carry, key_piece, value_piece, queries):
    maxima, denominator, accumulated = carry
    scaling = 1.0 / jnp.sqrt(jnp.float32(C))
    scores = (
        jnp.einsum("qc,kc->qk", queries, key_piece, preferred_element_type=jnp.float32) * scaling
    )
    newest = jnp.maximum(maxima, jnp.max(scores, axis=1))
    expo = jnp.exp(scores - newest[:, None])
    denominator = jnp.sum(expo, axis=1)
    accumulated = jnp.dot(
        expo.astype(jnp.bfloat16), value_piece, preferred_element_type=jnp.float32
    )
    return (newest, denominator, accumulated)


def local(
    latent,
    attn_gain,
    attn_shift,
    w_query,
    w_key,
    w_value,
    w_out,
    conv_gain,
    conv_shift,
    w_conv,
    conv_bias,
):
    local_rows = latent.shape[0]
    positions = latent.reshape(local_rows * W, C)
    normed = group_norm(positions.astype(jnp.float32), attn_gain, attn_shift).astype(jnp.bfloat16)
    queries = jnp.dot(normed, w_query, preferred_element_type=jnp.float32).astype(jnp.bfloat16)
    count_rows = positions.shape[0]
    start_carry = (
        jnp.full((count_rows,), -1e30, jnp.float32),
        jnp.zeros((count_rows,), jnp.float32),
        jnp.zeros((count_rows, C), jnp.float32),
    )
    piece = lax.all_gather(normed, "row", axis=0, tiled=True)
    key_piece = jnp.dot(piece, w_key, preferred_element_type=jnp.float32).astype(jnp.bfloat16)
    value_piece = jnp.dot(piece, w_value, preferred_element_type=jnp.float32).astype(jnp.bfloat16)
    maxima, denominator, accumulated = attend(start_carry, key_piece, value_piece, queries)
    attended = (accumulated / denominator[:, None]).astype(jnp.bfloat16)
    hidden = (
        positions.astype(jnp.float32) + jnp.dot(attended, w_out, preferred_element_type=jnp.float32)
    ).astype(jnp.bfloat16)
    activated = jax.nn.silu(group_norm(hidden.astype(jnp.float32), conv_gain, conv_shift)).astype(
        jnp.bfloat16
    )
    activated = activated.reshape(local_rows, W, C)
    bordered = with_halo(activated, (("row", 0),), 1)
    padded = jnp.pad(bordered, ((0, 0), (1, 1), (0, 0)))
    convolved = jnp.zeros((local_rows * W, C), jnp.float32)
    for row_tap in range(3):
        for col_tap in range(3):
            window = padded[row_tap : row_tap + local_rows, col_tap : col_tap + W].reshape(
                local_rows * W, C
            )
            convolved = convolved + jnp.dot(
                window, w_conv[row_tap, col_tap], preferred_element_type=jnp.float32
            )
    encoded = hidden.astype(jnp.float32) + (convolved + conv_bias)
    return encoded.astype(jnp.bfloat16).reshape(local_rows, W, C)


def solution(mesh):
    in_specs = (P(("img", "row"), None, None), P(), P(), P(), P(), P(), P(), P(), P(), P(), P())
    out_specs = P(("img", "row"), None, None)
    return jax.shard_map(local, mesh=mesh, in_specs=in_specs, out_specs=out_specs, check_vma=False)
```

profile of v0, /device:TPU:1, one launch (start us, length us, event | category | flops | bytes accessed | tf_op | source)
XLA Modules:
  0.0 157.1 jit_solution(7887998248014053439)
XLA Ops:
  6.5 1.3 convert_reduce_fusion.1
  7.8 0.1 reduce_sum.74
  7.9 0.1 reduce_sum.80
  8.0 0.1 reduce_sum.75
  8.1 0.1 reduce_sum.96
  8.2 0.1 pad_maximum_fusion.2
  8.3 16.8 %all_to_all.12 = f32[16,1,64]{2,1,0:T(1,128)S(1)} all-to-all(f32[16,1,64]{2,1,0:T(1,128)S(1)} %broadcast_in_dim.6), channel_id=1, replica_groups=mesh['img'=16,'row'=16] {'row'}, dimensions={0} | all-to-all | bytes 8192 | tf_op jit(solution)/shard_map/all_to_all | solution.py:16
  25.1 0.1 slice_multiply_fusion.1
  25.2 0.1 sub.40
  25.3 0.1 sub.41
  25.4 0.1 mul.68
  25.4 0.1 mul.69
  25.5 2.1 %fusion.31 = bf16[512,512]{1,0:T(8,128)(2,1)} fusion(bf16[4,128,512]{2,1,0:T(8,128)(2,1)} %param.11, f32[512]{0:T(512)} %param.13, f32[512]{0:T(512)} %param.12, f32[512]{0:T(512)S(1)} %mul.69, f32[512]{0:T(512)S(1)} %sub.41), kind=kLoop, calls=%fused_computation.46 | loop fusion | flops 1572864 | bytes 1056768 | tf_op jit(solution)/shard_map/convert_element_type | solution.py:96
  27.6 0.0 all-gather.2.cloned.1.call-update
  27.6 1.6 %convolution_convert_fusion.2 = bf16[512,512]{1,0:T(8,128)(2,1)S(1)} fusion(bf16[512,512]{1,0:T(8,128)(2,1)} %fusion.31, bf16[512,512]{1,0:T(8,128)(2,1)} %param.14), kind=kOutput, calls=%fused_computation.28 | convolution fusion | flops 268697600 | bytes 1572864 | tf_op jit(solution)/shard_map/dot_general | solution.py:97
  29.2 51.1 %all-gather.2.cloned.1.call-done = bf16[8192,512]{1,0:T(8,128)(2,1)} async-done(((bf16[512,512]{1,0:T(8,128)(2,1)}), bf16[8192,512]{1,0:T(8,128)(2,1)}) %all-gather.2.cloned.1.call-update) | async-done | bytes 8388624 | tf_op jit(solution)/shard_map/all_gather | solution.py:104
  80.4 14.5 %multiply_reduce_fusion = (f32[512]{0:T(512)S(1)}, f32[512,8192]{1,0:T(8,128)}) fusion(bf16[512,512]{1,0:T(8,128)(2,1)S(1)} %convolution_convert_fusion.2, bf16[8192,512]{1,0:T(8,128)(2,1)} %all-gather.2.cloned.1.call-done, bf16[512,512]{1,0:T(8,128)(2,1)S(1)} %copy-done), kind=kOutput, calls=%fused_computation.1 | convolution fusion | flops 8602517504 | bytes 26216448 | tf_op jit(solution)/shard_map/qc,kc->qk/dot_general | solution.py:70
  94.9 8.7 %fusion = f32[512]{0:T(512)S(1)} fusion(f32[512,8192]{1,0:T(8,128)} %get-tuple-element.24, f32[512]{0:T(512)S(1)} %broadcast_maximum_fusion), kind=kLoop, calls=%fused_computation.2 | loop fusion | flops 12582400 | bytes 16781312 | tf_op jit(solution)/shard_map/reduce_sum | solution.py:74
  103.6 17.2 %fusion.15 = bf16[512,512]{1,0:T(8,128)(2,1)S(1)} fusion(bf16[8192,512]{1,0:T(8,128)(2,1)} %all-gather.2.cloned.1.call-done, bf16[512,512]{1,0:T(8,128)(2,1)S(1)} %copy-done.5, f32[512,8192]{1,0:T(8,128)} %get-tuple-element.24, f32[512]{0:T(512)S(1)} %broadcast_maximum_fusion, f32[512]{0:T(512)S(1)} %fusion), kind=kOutput, calls=%fused_computation.31 | convolution fusion | flops 8607236096 | bytes 26218496 | tf_op jit(solution)/shard_map/dot_general | solution.py:75
  120.8 0.5 convert_reduce_fusion
  121.3 0.1 reduce_sum.100
  121.4 0.3 reduce_sum.101
  121.7 0.1 reduce_sum.103
  121.8 0.1 reduce_sum.104
  121.9 0.1 pad_maximum_fusion.3
  122.0 11.4 %all_to_all.13 = f32[16,1,64]{2,1,0:T(1,128)S(1)} all-to-all(f32[16,1,64]{2,1,0:T(1,128)S(1)} %broadcast_in_dim.8), channel_id=1, replica_groups=mesh['img'=16,'row'=16] {'row'}, dimensions={0} | all-to-all | bytes 8192 | tf_op jit(solution)/shard_map/all_to_all | solution.py:16
  133.4 0.1 slice_multiply_fusion
  133.5 0.1 sub.47
  133.6 0.1 sub.48
  133.7 0.1 mul.78
  133.7 0.1 mul.79
  133.8 0.4 fusion.27
  134.2 2.7 %collective-permute-start = (bf16[1,128,512]{2,1,0:T(8,128)(2,1)S(1)}, bf16[1,128,512]{2,1,0:T(8,128)(2,1)S(1)}, u32[]{:S(2)}, u32[]{:S(2)}) collective-permute-start(bf16[1,128,512]{2,1,0:T(8,128)(2,1)S(1)} %get-tuple-element.17), channel_id=1, source_target_pairs={{0,1},{1,2},{2,3},{3,4},{4,5},{5,6},{6,7},{7,8},{8,9},{9,10},{10,1... | collective-permute-start | bytes 393224 | tf_op jit(solution)/shard_map/ppermute | solution.py:40
  137.0 1.9 %collective-permute-start.1 = (bf16[1,128,512]{2,1,0:T(8,128)(2,1)S(1)}, bf16[1,128,512]{2,1,0:T(8,128)(2,1)S(1)}, u32[]{:S(2)}, u32[]{:S(2)}) collective-permute-start(bf16[1,128,512]{2,1,0:T(8,128)(2,1)S(1)} %get-tuple-element.18), channel_id=1, source_target_pairs={{1,0},{2,1},{3,2},{4,3},{5,4},{6,5},{7,6},{8,7},{9,8},{10,9},{11,1... | collective-permute-start | bytes 393224 | tf_op jit(solution)/shard_map/ppermute | solution.py:42
  138.9 4.3 %collective-permute-done.1 = bf16[1,128,512]{2,1,0:T(8,128)(2,1)S(1)} collective-permute-done((bf16[1,128,512]{2,1,0:T(8,128)(2,1)S(1)}, bf16[1,128,512]{2,1,0:T(8,128)(2,1)S(1)}, u32[]{:S(2)}, u32[]{:S(2)}) %collective-permute-start.1) | collective-permute-done | bytes 131104 | tf_op jit(solution)/shard_map/ppermute | solution.py:42
  143.3 0.2 fusion.36
  143.5 0.4 fusion.58
  143.9 1.7 %fusion.46 = f32[512,512]{1,0:T(8,128)S(1)} fusion(bf16[512,512]{1,0:T(8,128)(2,1)S(1)} %bitcast.82, bf16[3,3,512,512]{3,2,1,0:T(8,128)(2,1)} %param.20), kind=kOutput, calls=%fused_computation.65 | convolution fusion | flops 268435456 | bytes 2097152 | tf_op jit(solution)/shard_map/dot_general | solution.py:124
  145.6 0.1 pad_maximum_fusion
  145.7 0.1 slice-done.1
  145.8 0.4 convolution_add_fusion.6
  146.3 0.4 convolution_add_fusion.5
  146.7 0.4 convolution_add_fusion.4
  147.2 0.4 convolution_add_fusion.3
  147.6 0.4 fusion.37
  148.1 0.4 convolution_add_fusion.2
  148.5 0.4 convolution_add_fusion.1
  149.0 1.3 fusion.10
  (26 shorter events, 0.1 us)
Async XLA Ops:
  6.5 73.8 %copy-start = (bf16[512,512]{1,0:T(8,128)(2,1)S(1)}, bf16[512,512]{1,0:T(8,128)(2,1)}, u32[]{:S(2)}) copy-start(bf16[512,512]{1,0:T(8,128)(2,1)} %param.15) | copy-start | bytes 1572868
  6.5 73.8 %all-gather.2.cloned.1.call-start = ((), (), s32[]{:S(2)}) async-start(), calls=%async_computation.2 | async-start | bytes 8912896 | tf_op jit(solution)/shard_map/all_gather | solution.py:104
  94.9 8.7 %copy-start.5 = (bf16[512,512]{1,0:T(8,128)(2,1)S(1)}, bf16[512,512]{1,0:T(8,128)(2,1)}, u32[]{:S(2)}) copy-start(bf16[512,512]{1,0:T(8,128)(2,1)} %param.16) | copy-start | bytes 1572868
  103.6 17.2 %copy-start.1 = (bf16[4,128,512]{2,1,0:T(8,128)(2,1)S(1)}, bf16[4,128,512]{2,1,0:T(8,128)(2,1)}, u32[]{:S(2)}) copy-start(bf16[4,128,512]{2,1,0:T(8,128)(2,1)} %param.11) | copy-start | bytes 1572868
  103.6 17.2 %copy-start.6 = (bf16[512,512]{1,0:T(8,128)(2,1)S(1)}, bf16[512,512]{1,0:T(8,128)(2,1)}, u32[]{:S(2)}) copy-start(bf16[512,512]{1,0:T(8,128)(2,1)} %param.17) | copy-start | bytes 1572868
  103.6 30.2 %copy-start.2 = (f32[512]{0:T(512)S(1)}, f32[512]{0:T(512)}, u32[]{:S(2)}) copy-start(f32[512]{0:T(512)} %param.19) | copy-start | bytes 6148
  103.6 30.2 %copy-start.3 = (f32[512]{0:T(512)S(1)}, f32[512]{0:T(512)}, u32[]{:S(2)}) copy-start(f32[512]{0:T(512)} %param.18) | copy-start | bytes 6148
  120.8 24.9 %slice-start = ((s8[4718592]{0:T(1024)(128)(4,1)}), s8[524288]{0:T(1024)(128)(4,1)S(1)}, s32[]{:S(2)}) async-start(s8[4718592]{0:T(1024)(128)(4,1)} %bitcast.74), calls=%async_computation.3 | async-start | bytes 1048576
  134.2 4.7 %collective-permute-start = (bf16[1,128,512]{2,1,0:T(8,128)(2,1)S(1)}, bf16[1,128,512]{2,1,0:T(8,128)(2,1)S(1)}, u32[]{:S(2)}, u32[]{:S(2)}) collective-permute-start(bf16[1,128,512]{2,1,0:T(8,128)(2,1)S(1)} %get-tuple-element.17), channel_id=1, source_target_pairs={{0,1},{1,2},{2,3},{3,4},{4,5},{5,6},{6,7},{7,8},{8,9},{9,10},{10,1... | collective-permute-start | bytes 393224 | tf_op jit(solution)/shard_map/ppermute | solution.py:40
  137.0 6.3 %collective-permute-start.1 = (bf16[1,128,512]{2,1,0:T(8,128)(2,1)S(1)}, bf16[1,128,512]{2,1,0:T(8,128)(2,1)S(1)}, u32[]{:S(2)}, u32[]{:S(2)}) collective-permute-start(bf16[1,128,512]{2,1,0:T(8,128)(2,1)S(1)} %get-tuple-element.18), channel_id=1, source_target_pairs={{1,0},{2,1},{3,2},{4,3},{5,4},{6,5},{7,6},{8,7},{9,8},{10,9},{11,1... | collective-permute-start | bytes 393224 | tf_op jit(solution)/shard_map/ppermute | solution.py:42
  143.5 2.3 %slice-start.1 = ((s8[4718592]{0:T(1024)(128)(4,1)}), s8[4194304]{0:T(1024)(128)(4,1)S(1)}, s32[]{:S(2)}) async-start(s8[4718592]{0:T(1024)(128)(4,1)} %bitcast.74), calls=%async_computation.4 | async-start | bytes 8388608
  146.3 2.7 %copy-start.4 = (f32[512]{0:T(512)S(1)}, f32[512]{0:T(512)}, u32[]{:S(2)}) copy-start(f32[512]{0:T(512)} %param.21) | copy-start | bytes 6148
Sparse Core Ops, SparseCore 0:
  27.7 52.6 all-gather.1
where the time goes:
time: 157 us
  waiting for transfers between devices  55.5 us (35%)
  matrix products  39.9 us (25%)
  blocking collectives  28.2 us (18%)
  other arithmetic  13.7 us (9%)
  between operations  13.6 us (9%)
  starting transfers between devices  4.64 us (3%)
    all_gather x1, waiting for transfers between devices, local(): piece = lax.all_gather(normed, 'row', axis=0, tiled=True)  51.1 us
    all_to_all x2, blocking collectives, copy_for_each(): return lax.all_to_all(copies, axis, split_axis=0, concat_axis=0, tiled=True)  28.2 us
    dot_general x1, matrix products, attend(): jnp.dot(expo.astype(jnp.bfloat16), value_piece, preferred_element_type=jn...  17.2 us
    dot_general x1, matrix products, attend(): jnp.einsum('qc,kc->qk', queries, key_piece, preferred_element_type=jnp.fl...  14.5 us
    reduce_sum x1, other arithmetic, attend(): denominator = jnp.sum(expo, axis=1)  8.68 us
    dot_general x9, matrix products, local(): jnp.dot(window, w_conv[row_tap, col_tap], preferred_element_type=jnp.floa...  6.07 us
    ppermute x1, waiting for transfers between devices, with_halo(): lax.ppermute(head, axis, [((i + 1) % count, i) for i in range(ends)])  4.35 us
  transfers between devices with their start and end apart: 3, of which 2 were waited for; matrix products, arithmetic and copies ran while one was open for 1% of the time, Pallas kernels for 0%

commit v1 on v0

v1 whole, which is shorter than its diff:
```python
import functools

import jax
import jax.numpy as jnp
from jax import lax
from jax.experimental import pallas as pl
from jax.experimental.pallas import tpu as pltpu
from jax.sharding import PartitionSpec as P

MESH = pl.DeviceIdType.MESH
C = 512
GROUP = 16
W = 128
EPS = 1e-06
PIECE = 128
LOG2E = 1.4426950408889634
F32 = jnp.float32
BF16 = jnp.bfloat16


def group_total(x):
    lane = lax.broadcasted_iota(jnp.int32, x.shape, 1)
    width = x.shape[1]
    for s in (1, 2, 4, 8):
        up = pltpu.roll(x, s, 1)
        down = pltpu.roll(x, width - s, 1)
        x = x + jnp.where((lane // s) % 2 == 1, up, down)
    return x


def channel_stats(x):
    mean = jnp.sum(x, axis=0, keepdims=True) * (1.0 / x.shape[0])
    off = x - mean
    return mean, jnp.sum(off * off, axis=0, keepdims=True)


def affine(means, seconds, count, gain, shift):
    devices = means.shape[0]
    centre = group_total(
        jnp.broadcast_to(jnp.sum(means, axis=0, keepdims=True), (8, C))
    )[:1] * (1.0 / (devices * GROUP))
    off = means - centre
    second = jnp.sum(seconds + count * (off * off), axis=0, keepdims=True)
    spread = group_total(jnp.broadcast_to(second, (8, C)))[:1] * (1.0 / (devices * GROUP * count))
    a = lax.rsqrt(spread + EPS) * gain
    return a, shift - centre * a


def dot(x, y):
    return jnp.dot(x, y, preferred_element_type=F32)


def dot_t(x, y):
    return lax.dot_general(x, y, (((1,), (1,)), ((), ())), preferred_element_type=F32)


def kernel(
    n,
    lat,
    vecs,
    wq,
    wk,
    wv,
    wo,
    wc,
    out,
    gathered,
    vec,
    wq_v,
    wk_v,
    wv_v,
    wo_v,
    wc_v,
    q_v,
    m_v,
    l_v,
    acc_v,
    hid_v,
    halo_v,
    act_v,
    st1,
    st2,
    local_sem,
    ring_send,
    ring_recv,
    sib_send,
    sib_recv,
    st_send,
    st_recv,
    halo_send,
    halo_recv,
):
    me = lax.axis_index("row")
    chips = n // 2
    z, core = me // 2, me % 2
    sib = me + 1 - 2 * core
    count = lat.shape[0]
    parts = count // PIECE
    half = chips // 2
    steps = (half - 1) * parts + parts // 2
    nexts = (
        lax.rem(z + 1, chips) * 2 + core,
        lax.rem(z + chips - 1, chips) * 2 + core,
    )

    get_lat = pltpu.make_async_copy(lat, gathered.at[me], local_sem.at[0])
    get_lat.start()
    get_vec = pltpu.make_async_copy(vecs, vec, local_sem.at[1])
    get_vec.start()
    gets = []
    for i, (a, b) in enumerate(((wq, wq_v), (wk, wk_v), (wv, wv_v), (wo, wo_v), (wc, wc_v))):
        gets.append(pltpu.make_async_copy(a, b, local_sem.at[2 + i]))
        gets[-1].start()

    barrier = pltpu.get_barrier_semaphore()
    for k in range(1, n):
        pl.semaphore_signal(
            barrier, inc=1, device_id={"row": lax.rem(me + k, n)}, device_id_type=MESH
        )
    pl.semaphore_wait(barrier, n - 1)

    def place(d, r, c):
        hop = 1 + r // parts
        chip = lax.rem(z + chips - hop, chips) if d == 0 else lax.rem(z + hop, chips)
        j = lax.rem(r, parts) if d == 0 else lax.rem(r + parts // 2, parts)
        return chip * 2 + c, j * PIECE

    def piece(d, r, c):
        slot, at = place(d, r, c)
        return gathered.at[slot, pl.ds(pl.multiple_of(at, PIECE), PIECE)]

    def ring_copy(d, ref, t):
        return pltpu.make_async_remote_copy(
            src_ref=ref,
            dst_ref=ref,
            send_sem=ring_send.at[d, t],
            recv_sem=ring_recv.at[d, t],
            device_id={"row": nexts[d]},
            device_id_type=MESH,
        )

    def sib_copy(ref, d, r):
        return pltpu.make_async_remote_copy(
            src_ref=ref,
            dst_ref=ref,
            send_sem=sib_send.at[d, r],
            recv_sem=sib_recv.at[d, r],
            device_id={"row": sib},
            device_id_type=MESH,
        )

    def own_piece(d, t):
        j = t if d == 0 else (t + parts // 2) % parts
        return gathered.at[me, pl.ds(j * PIECE, PIECE)]

    get_lat.wait()
    for t in range(parts):
        for d in range(2):
            ring_copy(d, own_piece(d, t), t).start()
    own_to_sib = sib_copy(gathered.at[me], 0, steps)
    own_to_sib.start()

    def stats_copy(buf, which, k):
        return pltpu.make_async_remote_copy(
            src_ref=buf.at[0],
            dst_ref=buf.at[k],
            send_sem=st_send.at[which],
            recv_sem=st_recv.at[which],
            device_id={"row": lax.rem(me + k, n)},
            device_id_type=MESH,
        )

    def stats_all(buf, which):
        return pltpu.make_async_remote_copy(
            src_ref=buf.at[pl.ds(1, n - 1)],
            dst_ref=buf.at[pl.ds(1, n - 1)],
            send_sem=st_send.at[which],
            recv_sem=st_recv.at[which],
            device_id={"row": sib},
            device_id_type=MESH,
        )

    x = gathered[me].astype(F32)
    mean, second = channel_stats(x)
    st1[0, 0:1] = mean
    st1[0, 1:2] = second
    for k in range(1, n):
        stats_copy(st1, 0, k).start()

    gets[2].wait()
    gets[3].wait()
    wv_v[...] = dot(wv_v[...], wo_v[...]).astype(BF16)

    def comm(r):
        for d in range(2):
            ref = piece(d, r, core)
            ring_copy(d, ref, r).wait_recv()

            @pl.when(r < steps - parts)
            def _():
                ring_copy(d, ref, r + parts).start()

            sib_copy(ref, d, r).start()

    comm(0)
    comm(1)
    stats_all(st1, 0).wait_recv()
    get_vec.wait()
    a1, b1 = affine(st1[:, 0], st1[:, 1], float(count), vec[0:1], vec[1:2])
    gets[0].wait()
    gets[1].wait()
    normed = (x * a1 + b1).astype(BF16)
    queries = dot(normed, wq_v[...]).astype(BF16)
    q_v[...] = (dot_t(queries, wk_v[...]) * (a1 * (LOG2E / C**0.5))).astype(BF16)

    m_v[...] = jnp.full_like(m_v, -1e30)
    l_v[...] = jnp.zeros_like(l_v)
    acc_v[...] = jnp.zeros_like(acc_v)

    def attend(keys):
        s = dot_t(q_v[...], keys)
        old = m_v[...]
        new = jnp.maximum(old, jnp.max(s, axis=1, keepdims=True))
        scale = jnp.exp2(old - new)
        p = jnp.exp2(s - new[:, :1]).astype(BF16)
        wide = p.astype(F32)
        l_v[...] = l_v[...] * scale + sum(
            wide[:, i : i + 128] for i in range(0, wide.shape[1], 128)
        )
        acc_v[...] = acc_v[...] * scale[:, :1] + dot(p, keys)
        m_v[...] = new

    def attend_shard(slot):
        for i in range(0, count, 2 * PIECE):
            attend(gathered[slot, pl.ds(i, 2 * PIECE)])

    def attend_pieces(r, c):
        attend(jnp.concatenate([piece(0, r, c)[...], piece(1, r, c)[...]], axis=0))

    def compute(r):
        attend_pieces(r, core)
        for d in range(2):
            sib_copy(piece(d, r, 1 - core), d, r).wait_recv()
        attend_pieces(r, 1 - core)

    attend_shard(me)
    sib_copy(gathered.at[sib], 0, steps).wait_recv()
    attend_shard(sib)
    compute(0)

    def step(r, carry):
        compute(r - 1)
        comm(r)
        return carry

    lax.fori_loop(2, steps, step, 0)
    compute(steps - 1)

    total = jnp.sum(l_v[...], axis=1, keepdims=True)
    attended = (acc_v[...] / total * a1 + b1).astype(BF16)
    hidden = (gathered[me].astype(F32) + dot(attended, wv_v[...])).astype(BF16)
    hid_v[...] = hidden

    def halo_copy(i):
        rows = pl.ds(count - W, W) if i == 0 else pl.ds(0, W)
        peer = lax.rem(me + 1, n) if i == 0 else lax.rem(me + n - 1, n)
        return pltpu.make_async_remote_copy(
            src_ref=hid_v.at[rows],
            dst_ref=halo_v.at[i],
            send_sem=halo_send.at[i],
            recv_sem=halo_recv.at[i],
            device_id={"row": peer},
            device_id_type=MESH,
        )

    h = hidden.astype(F32)
    mean, second = channel_stats(h)
    st2[0, 0:1] = mean
    st2[0, 1:2] = second
    for k in range(1, n):
        stats_copy(st2, 1, k).start()
    for i in range(2):
        halo_copy(i).start()
    gets[4].wait()
    stats_all(st2, 1).wait_recv()
    a2, b2 = affine(st2[:, 0], st2[:, 1], float(count), vec[2:3], vec[3:4])
    for i in range(2):
        halo_copy(i).wait_recv()

    col = lax.broadcasted_iota(jnp.int32, (W, C), 0)
    image_rows = count // W
    for b in range(image_rows + 2):
        if b == 0:
            f = halo_v[0]
        elif b == image_rows + 1:
            f = halo_v[1]
        else:
            f = hid_v[pl.ds((b - 1) * W, W)]
        v = f.astype(F32) * a2 + b2
        v = v / (1.0 + jnp.exp(-v))
        if b == 0:
            v = jnp.where(me > 0, v, 0.0)
        elif b == image_rows + 1:
            v = jnp.where(me < n - 1, v, 0.0)
        rows = pl.ds(b * W, W)
        act_v[rows, pl.ds(0, C)] = jnp.where(col == 0, 0.0, pltpu.roll(v, 1, 0)).astype(BF16)
        act_v[rows, pl.ds(C, C)] = v.astype(BF16)
        act_v[rows, pl.ds(2 * C, C)] = jnp.where(col == W - 1, 0.0, pltpu.roll(v, W - 1, 0)).astype(
            BF16
        )

    conv = dot(act_v[pl.ds(0, count)], wc_v[0])
    conv = conv + dot(act_v[pl.ds(W, count)], wc_v[1])
    conv = conv + dot(act_v[pl.ds(2 * W, count)], wc_v[2])
    out[...] = (hid_v[...].astype(F32) + (conv + vec[4:5])).astype(BF16)

    for t in range(parts):
        for d in range(2):
            ring_copy(d, own_piece(d, t), t).wait_send()

    def drain(r, carry):
        for d in range(2):
            ref = piece(d, r, core)

            @pl.when(r < steps - parts)
            def _():
                ring_copy(d, ref, r + parts).wait_send()

            sib_copy(ref, d, r).wait_send()
        return carry

    lax.fori_loop(0, steps, drain, 0)
    own_to_sib.wait_send()
    stats_all(st1, 0).wait_send()
    stats_all(st2, 1).wait_send()
    for i in range(2):
        halo_copy(i).wait_send()


def local(n, latent, g1, s1, w_query, w_key, w_value, w_out, g2, s2, w_conv, bias):
    rows = latent.shape[0]
    count = rows * W
    parts = count // PIECE
    steps = (n // 4 - 1) * parts + parts // 2
    vecs = jnp.stack([g1, s1, g2, s2, bias, bias, bias, bias])
    dma = pltpu.SemaphoreType.DMA
    vm = pltpu.VMEM
    result = pl.pallas_call(
        functools.partial(kernel, n),
        name="block",
        out_shape=jax.ShapeDtypeStruct((count, C), BF16),
        in_specs=[pl.BlockSpec(memory_space=pl.ANY)] * 7,
        out_specs=pl.BlockSpec(memory_space=pltpu.VMEM),
        scratch_shapes=[
            vm((n, count, C), BF16),
            vm((8, C), F32),
            vm((C, C), BF16),
            vm((C, C), BF16),
            vm((C, C), BF16),
            vm((C, C), BF16),
            vm((3, 3 * C, C), BF16),
            vm((count, C), BF16),
            vm((count, 128), F32),
            vm((count, 128), F32),
            vm((count, C), F32),
            vm((count, C), BF16),
            vm((2, W, C), BF16),
            vm((count + 2 * W, 3 * C), BF16),
            vm((n, 2, C), F32),
            vm((n, 2, C), F32),
            dma((7,)),
            dma((2, steps)),
            dma((2, steps)),
            dma((2, steps + 1)),
            dma((2, steps + 1)),
            dma((2,)),
            dma((2,)),
            dma((2,)),
            dma((2,)),
        ],
        compiler_params=pltpu.CompilerParams(
            collective_id=0, has_side_effects=True, vmem_limit_bytes=60 * 1024 * 1024
        ),
    )(
        latent.reshape(count, C),
        vecs,
        w_query,
        w_key,
        w_value,
        w_out,
        w_conv.reshape(3, 3 * C, C),
    )
    return result.reshape(rows, W, C)


def solution(mesh):
    n = mesh.shape["row"]
    in_specs = (P(("img", "row"), None, None), P(), P(), P(), P(), P(), P(), P(), P(), P(), P())
    return jax.shard_map(
        functools.partial(local, n),
        mesh=mesh,
        in_specs=in_specs,
        out_specs=P(("img", "row"), None, None),
        check_vma=False,
    )
```

time: 157 us -> 77.9 us (0.50)
  Pallas kernels: 0 us -> 74.4 us
  waiting for transfers between devices: 55.5 us -> 0 us
  matrix products: 39.9 us -> 0 us
  blocking collectives: 28.2 us -> 0 us
  other arithmetic: 13.7 us -> 0 us
  between operations: 13.6 us -> 0.01 us
  starting transfers between devices: 4.64 us -> 0 us
  local copies, waits for them, and re-layouts: 1.52 us -> 3.33 us
    pallas_call x0 -> x1, Pallas kernels: none -> 74.4 us  [local(): pl.pallas_call(functools.partial(kernel, n), name='block', out_shape=jax....]
    all_gather x1 -> x0, waiting for transfers between devices: 51.1 us -> none  [local(): piece = lax.all_gather(normed, 'row', axis=0, tiled=True)]
    dot_general x13 -> x0, matrix products: 39.9 us -> none  [the longest x1 17.2 us: attend(): jnp.dot(expo.astype(jnp.bfloat16), value_piece, preferred_element_type=jn...]
    all_to_all x2 -> x0, blocking collectives: 28.2 us -> none  [copy_for_each(): return lax.all_to_all(copies, axis, split_axis=0, concat_axis=0, tiled=True)]
    reduce_sum x8 -> x0, other arithmetic: 10.6 us -> none  [the longest x1 8.68 us: attend(): denominator = jnp.sum(expo, axis=1)]
    ppermute x2 -> x0, starting transfers between devices: 4.64 us -> none  [the longest x1 2.72 us: with_halo(): lax.ppermute(tail, axis, [(i, (i + 1) % count) for i in range(ends)])]
    ppermute x2 -> x0, waiting for transfers between devices: 4.35 us -> none  [the longest x1 4.35 us: with_halo(): lax.ppermute(head, axis, [((i + 1) % count, i) for i in range(ends)])]
    convert_element_type x2 -> x0, other arithmetic: 2.43 us -> none  [the longest x1 2.06 us: local(): group_norm(positions.astype(jnp.float32), attn_gain, attn_shift)]
  transfers between devices with their start and end apart: 3 -> 0, of which waited for: 2 -> 0; matrix products, arithmetic and copies ran while one was open for 1% -> 0% of each run, Pallas kernels for 0% -> 0%
where the time goes in v1:
time: 77.9 us; the launch traced here: 77.7 us
  Pallas kernels  74.4 us (96%)
  local copies, waits for them, and re-layouts  3.33 us (4%)
    pallas_call x1, Pallas kernels, local(): pl.pallas_call(functools.partial(kernel, n), name='block', out_shape=jax....  74.4 us
    unnamed x1, local copies, waits for them, and re-layouts  1.87 us

profile of v1, /device:TPU:1, one launch (start us, length us, event | category | flops | bytes accessed | tf_op | source)
XLA Modules:
  0.0 77.7 jit_solution(2900492200524789109)
XLA Ops:
  0.0 1.5 %stack.26.vecs = f32[8,512]{1,0:T(8,128)} concatenate(f32[1,512]{1,0:T(1,128)} %bitcast.15, f32[1,512]{1,0:T(1,128)} %bitcast.16, f32[1,512]{1,0:T(1,128)} %bitcast.17, f32[1,512]{1,0:T(1,128)} %bitcast.18, f32[1,512]{1,0:T(1,128)} %bitcast.11, f32[1,512]{1,0:T(1,128)} %bitcast.12, f32[1,512]{1,0:T(1,128)} %bitcast.13, f32[1,512]{1,0:T(1,128)} %bitcast.14), dimensions={0} | concatenate | bytes 32768 | tf_op jit(solution)/shard_map/stack | solution.py:345
  1.5 74.4 %block.1 = bf16[512,512]{1,0:T(8,128)(2,1)} custom-call(bf16[512,512]{1,0:T(8,128)(2,1)} %bitcast.10, f32[8,512]{1,0:T(8,128)} %stack.26.vecs, bf16[512,512]{1,0:T(8,128)(2,1)} %wq.1, bf16[512,512]{1,0:T(8,128)(2,1)} %wk.1, bf16[512,512]{1,0:T(8,128)(2,1)} %wv.1, bf16[512,512]{1,0:T(8,128)(2,1)} %wo.1, bf16[3,1536,512]{2,1,0:T(8,128)(2,1)} %bitcast.8), custom_call_target="tpu_custom_call" | custom-call | tf_op jit(solution)/shard_map/block/pallas_call | solution.py:348
  75.8 1.9 %copy.13 = bf16[4,128,512]{2,1,0:T(8,128)(2,1)} copy(bf16[4,128,512]{2,1,0:T(8,128)(2,1)} %bitcast.9) | data formatting | bytes 1048576

commit v2 on v1

--- a/solution.py
+++ b/solution.py
@@ -34,16 +34,21 @@
     return mean, jnp.sum(off * off, axis=0, keepdims=True)
 
 
-def affine(means, seconds, count, gain, shift):
+def group_mean(mean):
+    return group_total(jnp.broadcast_to(mean, (8, C)))[:1] * (1.0 / GROUP)
+
+
+def affine(means, seconds, near, count, gain, shift):
     devices = means.shape[0]
-    centre = group_total(
-        jnp.broadcast_to(jnp.sum(means, axis=0, keepdims=True), (8, C))
-    )[:1] * (1.0 / (devices * GROUP))
-    off = means - centre
+    off = means - near
+    first = jnp.sum(off, axis=0, keepdims=True)
     second = jnp.sum(seconds + count * (off * off), axis=0, keepdims=True)
-    spread = group_total(jnp.broadcast_to(second, (8, C)))[:1] * (1.0 / (devices * GROUP * count))
-    a = lax.rsqrt(spread + EPS) * gain
-    return a, shift - centre * a
+    row = lax.broadcasted_iota(jnp.int32, (8, C), 0)
+    both = group_total(jnp.where(row == 0, first, second))
+    offset = both[0:1] * (1.0 / (devices * GROUP))
+    spread = both[1:2] * (1.0 / (devices * GROUP * count)) - offset * offset
+    a = lax.rsqrt(jnp.maximum(spread, 0.0) + EPS) * gain
+    return a, shift - (near + offset) * a
 
 
 def dot(x, y):
@@ -57,7 +62,11 @@
 def kernel(
     n,
     lat,
-    vecs,
+    g1,
+    s1,
+    g2,
+    s2,
+    bias,
     wq,
     wk,
     wv,
@@ -85,6 +94,7 @@
     ring_recv,
     sib_send,
     sib_recv,
+    heard,
     st_send,
     st_recv,
     halo_send,
@@ -102,22 +112,26 @@
         lax.rem(z + 1, chips) * 2 + core,
         lax.rem(z + chips - 1, chips) * 2 + core,
     )
+    near = (sib,) + nexts + tuple(peer + 1 - 2 * core for peer in nexts)
 
     get_lat = pltpu.make_async_copy(lat, gathered.at[me], local_sem.at[0])
     get_lat.start()
-    get_vec = pltpu.make_async_copy(vecs, vec, local_sem.at[1])
-    get_vec.start()
     gets = []
+    get_vecs = []
+    for i, a in enumerate((g1, s1, g2, s2, bias)):
+        get_vecs.append(pltpu.make_async_copy(a, vec.at[i], local_sem.at[7 + i]))
+        get_vecs[-1].start()
     for i, (a, b) in enumerate(((wq, wq_v), (wk, wk_v), (wv, wv_v), (wo, wo_v), (wc, wc_v))):
         gets.append(pltpu.make_async_copy(a, b, local_sem.at[2 + i]))
         gets[-1].start()
 
+    def greet(semaphore):
+        for peer in near:
+            pl.semaphore_signal(semaphore, inc=1, device_id={"row": peer}, device_id_type=MESH)
+
     barrier = pltpu.get_barrier_semaphore()
-    for k in range(1, n):
-        pl.semaphore_signal(
-            barrier, inc=1, device_id={"row": lax.rem(me + k, n)}, device_id_type=MESH
-        )
-    pl.semaphore_wait(barrier, n - 1)
+    greet(barrier)
+    pl.semaphore_wait(barrier, len(near))
 
     def place(d, r, c):
         hop = 1 + r // parts
@@ -159,6 +173,7 @@
             ring_copy(d, own_piece(d, t), t).start()
     own_to_sib = sib_copy(gathered.at[me], 0, steps)
     own_to_sib.start()
+    greet(heard.at[0])
 
     def stats_copy(buf, which, k):
         return pltpu.make_async_remote_copy(
@@ -180,12 +195,17 @@
             device_id_type=MESH,
         )
 
-    x = gathered[me].astype(F32)
-    mean, second = channel_stats(x)
+    mean, second = channel_stats(gathered[me].astype(F32))
     st1[0, 0:1] = mean
     st1[0, 1:2] = second
+    rounds = chips // 2 - 1
+    for k in range(rounds):
+        pl.semaphore_wait(heard.at[k], len(near))
+        if k + 1 < rounds:
+            greet(heard.at[k + 1])
     for k in range(1, n):
         stats_copy(st1, 0, k).start()
+    near1 = group_mean(mean)
 
     gets[2].wait()
     gets[3].wait()
@@ -205,11 +225,12 @@
     comm(0)
     comm(1)
     stats_all(st1, 0).wait_recv()
-    get_vec.wait()
-    a1, b1 = affine(st1[:, 0], st1[:, 1], float(count), vec[0:1], vec[1:2])
+    for g in get_vecs:
+        g.wait()
+    a1, b1 = affine(st1[:, 0], st1[:, 1], near1, float(count), vec[0], vec[1])
     gets[0].wait()
     gets[1].wait()
-    normed = (x * a1 + b1).astype(BF16)
+    normed = (gathered[me].astype(F32) * a1 + b1).astype(BF16)
     queries = dot(normed, wq_v[...]).astype(BF16)
     q_v[...] = (dot_t(queries, wk_v[...]) * (a1 * (LOG2E / C**0.5))).astype(BF16)
 
@@ -217,35 +238,34 @@
     l_v[...] = jnp.zeros_like(l_v)
     acc_v[...] = jnp.zeros_like(acc_v)
 
+    def wide(x, width):
+        return jnp.concatenate([x] * (width // 128), axis=1)
+
     def attend(keys):
-        s = dot_t(q_v[...], keys)
-        old = m_v[...]
-        new = jnp.maximum(old, jnp.max(s, axis=1, keepdims=True))
-        scale = jnp.exp2(old - new)
-        p = jnp.exp2(s - new[:, :1]).astype(BF16)
-        wide = p.astype(F32)
-        l_v[...] = l_v[...] * scale + sum(
-            wide[:, i : i + 128] for i in range(0, wide.shape[1], 128)
-        )
-        acc_v[...] = acc_v[...] * scale[:, :1] + dot(p, keys)
-        m_v[...] = new
-
-    def attend_shard(slot):
-        for i in range(0, count, 2 * PIECE):
-            attend(gathered[slot, pl.ds(i, 2 * PIECE)])
-
-    def attend_pieces(r, c):
-        attend(jnp.concatenate([piece(0, r, c)[...], piece(1, r, c)[...]], axis=0))
+        width = keys.shape[0]
+        halves = [pl.ds(i * (count // 2), count // 2) for i in range(2)]
+        scores = [dot_t(q_v[h], keys) for h in halves]
+        for h, s in zip(halves, scores):
+            old = m_v[h]
+            new = jnp.maximum(old, jnp.max(s, axis=1, keepdims=True))
+            scale = jnp.exp2(old - new)
+            p = jnp.exp2(s - wide(new, width)).astype(BF16)
+            back = p.astype(F32)
+            l_v[h] = l_v[h] * scale + sum(back[:, i : i + 128] for i in range(0, width, 128))
+            acc_v[h] = acc_v[h] * wide(scale, C) + dot(p, keys)
+            m_v[h] = new
+
+    def pieces(r, c):
+        return [piece(0, r, c)[...], piece(1, r, c)[...]]
 
     def compute(r):
-        attend_pieces(r, core)
         for d in range(2):
             sib_copy(piece(d, r, 1 - core), d, r).wait_recv()
-        attend_pieces(r, 1 - core)
-
-    attend_shard(me)
+        attend(jnp.concatenate(pieces(r, core) + pieces(r, 1 - core), axis=0))
+
+    attend(gathered[me])
     sib_copy(gathered.at[sib], 0, steps).wait_recv()
-    attend_shard(sib)
+    attend(gathered[sib])
     compute(0)
 
     def step(r, carry):
@@ -254,10 +274,13 @@
         return carry
 
     lax.fori_loop(2, steps, step, 0)
-    compute(steps - 1)
+    attend(jnp.concatenate(pieces(steps - 1, core), axis=0))
+    for d in range(2):
+        sib_copy(piece(d, steps - 1, 1 - core), d, steps - 1).wait_recv()
+    attend(jnp.concatenate(pieces(steps - 1, 1 - core), axis=0))
 
     total = jnp.sum(l_v[...], axis=1, keepdims=True)
-    attended = (acc_v[...] / total * a1 + b1).astype(BF16)
+    attended = (acc_v[...] * (1.0 / total) * a1 + b1).astype(BF16)
     hidden = (gathered[me].astype(F32) + dot(attended, wv_v[...])).astype(BF16)
     hid_v[...] = hidden
 
@@ -281,9 +304,10 @@
         stats_copy(st2, 1, k).start()
     for i in range(2):
         halo_copy(i).start()
+    near2 = group_mean(mean)
     gets[4].wait()
     stats_all(st2, 1).wait_recv()
-    a2, b2 = affine(st2[:, 0], st2[:, 1], float(count), vec[2:3], vec[3:4])
+    a2, b2 = affine(st2[:, 0], st2[:, 1], near2, float(count), vec[2], vec[3])
     for i in range(2):
         halo_copy(i).wait_recv()
 
@@ -312,7 +336,7 @@
     conv = dot(act_v[pl.ds(0, count)], wc_v[0])
     conv = conv + dot(act_v[pl.ds(W, count)], wc_v[1])
     conv = conv + dot(act_v[pl.ds(2 * W, count)], wc_v[2])
-    out[...] = (hid_v[...].astype(F32) + (conv + vec[4:5])).astype(BF16)
+    out[...] = (hid_v[...].astype(F32) + (conv + vec[4])).astype(BF16)
 
     for t in range(parts):
         for d in range(2):
@@ -342,18 +366,17 @@
     count = rows * W
     parts = count // PIECE
     steps = (n // 4 - 1) * parts + parts // 2
-    vecs = jnp.stack([g1, s1, g2, s2, bias, bias, bias, bias])
     dma = pltpu.SemaphoreType.DMA
     vm = pltpu.VMEM
     result = pl.pallas_call(
         functools.partial(kernel, n),
         name="block",
         out_shape=jax.ShapeDtypeStruct((count, C), BF16),
-        in_specs=[pl.BlockSpec(memory_space=pl.ANY)] * 7,
+        in_specs=[pl.BlockSpec(memory_space=pl.ANY)] * 11,
         out_specs=pl.BlockSpec(memory_space=pltpu.VMEM),
         scratch_shapes=[
             vm((n, count, C), BF16),
-            vm((8, C), F32),
+            vm((5, 1, C), F32),
             vm((C, C), BF16),
             vm((C, C), BF16),
             vm((C, C), BF16),
@@ -368,11 +391,12 @@
             vm((count + 2 * W, 3 * C), BF16),
             vm((n, 2, C), F32),
             vm((n, 2, C), F32),
-            dma((7,)),
+            dma((12,)),
             dma((2, steps)),
             dma((2, steps)),
             dma((2, steps + 1)),
             dma((2, steps + 1)),
+            pltpu.SemaphoreType.REGULAR((n // 4 - 1,)),
             dma((2,)),
             dma((2,)),
             dma((2,)),
@@ -383,7 +407,7 @@
         ),
     )(
         latent.reshape(count, C),
-        vecs,
+        *(v.reshape(1, C) for v in (g1, s1, g2, s2, bias)),
         w_query,
         w_key,
         w_value,

time: 77.9 us -> 66.6 us (0.85)
  Pallas kernels: 74.4 us -> 64.6 us
  local copies, waits for them, and re-layouts: 3.33 us -> 1.87 us
    pallas_call x1, Pallas kernels: 74.4 us -> 64.6 us  [local(): pl.pallas_call(functools.partial(kernel, n), name='block', out_shape=jax....]
    another operation x1 -> x0, local copies, waits for them, and re-layouts: 1.46 us -> none  [local(): vecs = jnp.stack([g1, s1, g2, s2, bias, bias, bias, bias])]
where the time goes in v2:
time: 66.6 us; the launch traced here: 66.5 us
  Pallas kernels  64.6 us (97%)
  local copies, waits for them, and re-layouts  1.87 us (3%)
    pallas_call x1, Pallas kernels, local(): pl.pallas_call(functools.partial(kernel, n), name='block', out_shape=jax....  64.6 us
    unnamed x1, local copies, waits for them, and re-layouts  1.87 us

profile of v2, /device:TPU:1, one launch (start us, length us, event | category | flops | bytes accessed | tf_op | source)
XLA Modules:
  0.0 66.5 jit_solution(1085200626342751872)
XLA Ops:
  0.0 64.6 %block.1 = bf16[512,512]{1,0:T(8,128)(2,1)} custom-call(bf16[512,512]{1,0:T(8,128)(2,1)} %bitcast.10, f32[1,512]{1,0:T(1,128)} %bitcast.11, f32[1,512]{1,0:T(1,128)} %bitcast.12, f32[1,512]{1,0:T(1,128)} %bitcast.13, f32[1,512]{1,0:T(1,128)} %bitcast.14, f32[1,512]{1,0:T(1,128)} %bitcast.15, bf16[512,512]{1,0:T(8,128)(2,1)} %wq.1, bf16[512,512]{1,0:T(8,128)(2,1)} %wk.1, ...), custom_call_target="tpu_custom_call" | custom-call | tf_op jit(solution)/shard_map/block/pallas_call | solution.py:371
  64.6 1.9 %copy.13 = bf16[4,128,512]{2,1,0:T(8,128)(2,1)} copy(bf16[4,128,512]{2,1,0:T(8,128)(2,1)} %bitcast.9) | data formatting | bytes 1048576

commit v3 on v2

--- a/solution.py
+++ b/solution.py
@@ -34,21 +34,44 @@
     return mean, jnp.sum(off * off, axis=0, keepdims=True)
 
 
-def group_mean(mean):
-    return group_total(jnp.broadcast_to(mean, (8, C)))[:1] * (1.0 / GROUP)
-
-
-def affine(means, seconds, near, count, gain, shift):
+def tiles(row):
+    at = lax.broadcasted_iota(jnp.int32, (8, 128), 0) % (C // 128)
+    out = jnp.broadcast_to(row[:, :128], (8, 128))
+    for k in range(1, C // 128):
+        out = jnp.where(at == k, row[:, 128 * k : 128 * (k + 1)], out)
+    return out
+
+
+def line(x):
+    lane = lax.broadcasted_iota(jnp.int32, (8, 128), 1) % GROUP
+    at = lax.broadcasted_iota(jnp.int32, (8, 128), 0)
+    return jnp.sum(jnp.where(lane == at, x, 0.0), axis=0, keepdims=True)
+
+
+def group_stats(mean, second, count):
+    mean, second = tiles(mean), tiles(second)
+    centre = group_total(mean) * (1.0 / GROUP)
+    off = mean - centre
+    return line(centre), line(group_total(second + count * (off * off)))
+
+
+def affine(means, seconds, count, gain, shift):
     devices = means.shape[0]
-    off = means - near
-    first = jnp.sum(off, axis=0, keepdims=True)
-    second = jnp.sum(seconds + count * (off * off), axis=0, keepdims=True)
-    row = lax.broadcasted_iota(jnp.int32, (8, C), 0)
-    both = group_total(jnp.where(row == 0, first, second))
-    offset = both[0:1] * (1.0 / (devices * GROUP))
-    spread = both[1:2] * (1.0 / (devices * GROUP * count)) - offset * offset
-    a = lax.rsqrt(jnp.maximum(spread, 0.0) + EPS) * gain
-    return a, shift - (near + offset) * a
+    centre = jnp.sum(means, axis=0, keepdims=True) * (1.0 / devices)
+    off = means - centre
+    size = count * GROUP
+    second = jnp.sum(seconds + size * (off * off), axis=0, keepdims=True)
+    scale = lax.rsqrt(second * (1.0 / (devices * size)) + EPS)
+    at = lax.broadcasted_iota(jnp.int32, (8, 128), 0)
+    lane = lax.broadcasted_iota(jnp.int32, (8, 128), 1) % GROUP
+    both = jnp.where(at < C // 128, centre, scale)
+    both = group_total(jnp.where(lane == at % (C // 128), both, 0.0))
+    centre, scale = (
+        jnp.concatenate([both[k : k + 1] for k in range(first, first + C // 128)], axis=1)
+        for first in (0, C // 128)
+    )
+    a = scale * gain
+    return a, shift - centre * a
 
 
 def dot(x, y):
@@ -196,6 +219,7 @@
         )
 
     mean, second = channel_stats(gathered[me].astype(F32))
+    mean, second = group_stats(mean, second, float(count))
     st1[0, 0:1] = mean
     st1[0, 1:2] = second
     rounds = chips // 2 - 1
@@ -205,7 +229,6 @@
             greet(heard.at[k + 1])
     for k in range(1, n):
         stats_copy(st1, 0, k).start()
-    near1 = group_mean(mean)
 
     gets[2].wait()
     gets[3].wait()
@@ -222,12 +245,12 @@
 
             sib_copy(ref, d, r).start()
 
-    comm(0)
-    comm(1)
+    for r in range(parts):
+        comm(r)
     stats_all(st1, 0).wait_recv()
     for g in get_vecs:
         g.wait()
-    a1, b1 = affine(st1[:, 0], st1[:, 1], near1, float(count), vec[0], vec[1])
+    a1, b1 = affine(st1[:, 0], st1[:, 1], float(count), vec[0], vec[1])
     gets[0].wait()
     gets[1].wait()
     normed = (gathered[me].astype(F32) * a1 + b1).astype(BF16)
@@ -266,14 +289,14 @@
     attend(gathered[me])
     sib_copy(gathered.at[sib], 0, steps).wait_recv()
     attend(gathered[sib])
-    compute(0)
+    lax.fori_loop(0, parts - 1, lambda r, carry: (compute(r), carry)[1], 0)
 
     def step(r, carry):
         compute(r - 1)
         comm(r)
         return carry
 
-    lax.fori_loop(2, steps, step, 0)
+    lax.fori_loop(parts, steps, step, 0)
     attend(jnp.concatenate(pieces(steps - 1, core), axis=0))
     for d in range(2):
         sib_copy(piece(d, steps - 1, 1 - core), d, steps - 1).wait_recv()
@@ -298,16 +321,16 @@
 
     h = hidden.astype(F32)
     mean, second = channel_stats(h)
+    mean, second = group_stats(mean, second, float(count))
     st2[0, 0:1] = mean
     st2[0, 1:2] = second
     for k in range(1, n):
         stats_copy(st2, 1, k).start()
     for i in range(2):
         halo_copy(i).start()
-    near2 = group_mean(mean)
     gets[4].wait()
     stats_all(st2, 1).wait_recv()
-    a2, b2 = affine(st2[:, 0], st2[:, 1], near2, float(count), vec[2], vec[3])
+    a2, b2 = affine(st2[:, 0], st2[:, 1], float(count), vec[2], vec[3])
     for i in range(2):
         halo_copy(i).wait_recv()
 
@@ -389,8 +412,8 @@
             vm((count, C), BF16),
             vm((2, W, C), BF16),
             vm((count + 2 * W, 3 * C), BF16),
-            vm((n, 2, C), F32),
-            vm((n, 2, C), F32),
+            vm((n, 2, 128), F32),
+            vm((n, 2, 128), F32),
             dma((12,)),
             dma((2, steps)),
             dma((2, steps)),

time: 66.6 us -> 64 us (0.961)
  Pallas kernels: 64.6 us -> 62 us
    pallas_call x1, Pallas kernels: 64.6 us -> 62 us  [local(): pl.pallas_call(functools.partial(kernel, n), name='block', out_shape=jax....]
where the time goes in v3:
time: 64 us; the launch traced here: 63.8 us
  Pallas kernels  62 us (97%)
  local copies, waits for them, and re-layouts  1.87 us (3%)
    pallas_call x1, Pallas kernels, local(): pl.pallas_call(functools.partial(kernel, n), name='block', out_shape=jax....  62 us
    unnamed x1, local copies, waits for them, and re-layouts  1.87 us

profile of v3, /device:TPU:1, one launch (start us, length us, event | category | flops | bytes accessed | tf_op | source)
XLA Modules:
  0.0 63.8 jit_solution(6758228065900837621)
XLA Ops:
  0.0 62.0 %block.1 = bf16[512,512]{1,0:T(8,128)(2,1)} custom-call(bf16[512,512]{1,0:T(8,128)(2,1)} %bitcast.10, f32[1,512]{1,0:T(1,128)} %bitcast.11, f32[1,512]{1,0:T(1,128)} %bitcast.12, f32[1,512]{1,0:T(1,128)} %bitcast.13, f32[1,512]{1,0:T(1,128)} %bitcast.14, f32[1,512]{1,0:T(1,128)} %bitcast.15, bf16[512,512]{1,0:T(8,128)(2,1)} %wq.1, bf16[512,512]{1,0:T(8,128)(2,1)} %wk.1, ...), custom_call_target="tpu_custom_call" | custom-call | tf_op jit(solution)/shard_map/block/pallas_call | solution.py:394
  62.0 1.9 %copy.13 = bf16[4,128,512]{2,1,0:T(8,128)(2,1)} copy(bf16[4,128,512]{2,1,0:T(8,128)(2,1)} %bitcast.9) | data formatting | bytes 1048576

commit v4 on v3

--- a/solution.py
+++ b/solution.py
@@ -53,6 +53,24 @@
     centre = group_total(mean) * (1.0 / GROUP)
     off = mean - centre
     return line(centre), line(group_total(second + count * (off * off)))
+
+
+def shifted_stats(x, near, count):
+    off = x - near
+    first = jnp.sum(off, axis=0, keepdims=True)
+    second = jnp.sum(off * off, axis=0, keepdims=True)
+    at = lax.broadcasted_iota(jnp.int32, (8, 128), 0)
+    total = group_total(jnp.where(at < C // 128, tiles(first), tiles(second)))
+    lane = lax.broadcasted_iota(jnp.int32, (8, 128), 1) % GROUP
+    mine = jnp.where(lane == at % (C // 128), total, 0.0)
+    first = jnp.sum(jnp.where(at < C // 128, mine, 0.0), axis=0, keepdims=True)
+    second = jnp.sum(jnp.where(at < C // 128, 0.0, mine), axis=0, keepdims=True)
+    offset = first * (1.0 / (GROUP * count))
+    lanes = lax.broadcasted_iota(jnp.int32, (1, 128), 1) % GROUP
+    base = near[:, :128]
+    for k in range(1, C // 128):
+        base = jnp.where(lanes == k, near[:, 128 * k : 128 * (k + 1)], base)
+    return base + offset, jnp.maximum(second - first * offset, 0.0)
 
 
 def affine(means, seconds, count, gain, shift):
@@ -71,7 +89,7 @@
         for first in (0, C // 128)
     )
     a = scale * gain
-    return a, shift - centre * a
+    return a, shift - centre * a, centre
 
 
 def dot(x, y):
@@ -139,15 +157,6 @@
 
     get_lat = pltpu.make_async_copy(lat, gathered.at[me], local_sem.at[0])
     get_lat.start()
-    gets = []
-    get_vecs = []
-    for i, a in enumerate((g1, s1, g2, s2, bias)):
-        get_vecs.append(pltpu.make_async_copy(a, vec.at[i], local_sem.at[7 + i]))
-        get_vecs[-1].start()
-    for i, (a, b) in enumerate(((wq, wq_v), (wk, wk_v), (wv, wv_v), (wo, wo_v), (wc, wc_v))):
-        gets.append(pltpu.make_async_copy(a, b, local_sem.at[2 + i]))
-        gets[-1].start()
-
     def greet(semaphore):
         for peer in near:
             pl.semaphore_signal(semaphore, inc=1, device_id={"row": peer}, device_id_type=MESH)
@@ -197,6 +206,22 @@
     own_to_sib = sib_copy(gathered.at[me], 0, steps)
     own_to_sib.start()
     greet(heard.at[0])
+    gets = []
+    get_vecs = []
+    for i, a in enumerate((g1, s1, g2, s2, bias)):
+        get_vecs.append(pltpu.make_async_copy(a, vec.at[i], local_sem.at[7 + i]))
+        get_vecs[-1].start()
+    for i, (a, b) in enumerate(((wq, wq_v), (wk, wk_v), (wv, wv_v), (wo, wo_v))):
+        gets.append(pltpu.make_async_copy(a, b, local_sem.at[2 + i]))
+        gets[-1].start()
+    get_taps = [
+        pltpu.make_async_copy(wc.at[:, tap], wc_v.at[tap], local_sem.at[12 + tap]) for tap in range(3)
+    ]
+    for g in get_taps:
+        g.start()
+
+
+    farthest = sorted(range(1, n), key=lambda k: abs(k - n // 2))
 
     def stats_copy(buf, which, k):
         return pltpu.make_async_remote_copy(
@@ -227,7 +252,7 @@
         pl.semaphore_wait(heard.at[k], len(near))
         if k + 1 < rounds:
             greet(heard.at[k + 1])
-    for k in range(1, n):
+    for k in farthest:
         stats_copy(st1, 0, k).start()
 
     gets[2].wait()
@@ -250,7 +275,7 @@
     stats_all(st1, 0).wait_recv()
     for g in get_vecs:
         g.wait()
-    a1, b1 = affine(st1[:, 0], st1[:, 1], float(count), vec[0], vec[1])
+    a1, b1, centre1 = affine(st1[:, 0], st1[:, 1], float(count), vec[0], vec[1])
     gets[0].wait()
     gets[1].wait()
     normed = (gathered[me].astype(F32) * a1 + b1).astype(BF16)
@@ -319,24 +344,40 @@
             device_id_type=MESH,
         )
 
-    h = hidden.astype(F32)
-    mean, second = channel_stats(h)
-    mean, second = group_stats(mean, second, float(count))
+    mean, second = shifted_stats(hidden.astype(F32), centre1, float(count))
     st2[0, 0:1] = mean
     st2[0, 1:2] = second
-    for k in range(1, n):
+    for k in farthest:
         stats_copy(st2, 1, k).start()
     for i in range(2):
         halo_copy(i).start()
-    gets[4].wait()
+    for t in range(parts):
+        for d in range(2):
+            ring_copy(d, own_piece(d, t), t).wait_send()
+
+    def drain(r, carry):
+        for d in range(2):
+            ref = piece(d, r, core)
+
+            @pl.when(r < steps - parts)
+            def _():
+                ring_copy(d, ref, r + parts).wait_send()
+
+            sib_copy(ref, d, r).wait_send()
+        return carry
+
+    lax.fori_loop(0, steps, drain, 0)
+    for g in get_taps:
+        g.wait()
     stats_all(st2, 1).wait_recv()
-    a2, b2 = affine(st2[:, 0], st2[:, 1], float(count), vec[2], vec[3])
+    a2, b2, _ = affine(st2[:, 0], st2[:, 1], float(count), vec[2], vec[3])
     for i in range(2):
         halo_copy(i).wait_recv()
 
     col = lax.broadcasted_iota(jnp.int32, (W, C), 0)
     image_rows = count // W
-    for b in range(image_rows + 2):
+
+    def activate(b):
         if b == 0:
             f = halo_v[0]
         elif b == image_rows + 1:
@@ -349,34 +390,34 @@
             v = jnp.where(me > 0, v, 0.0)
         elif b == image_rows + 1:
             v = jnp.where(me < n - 1, v, 0.0)
-        rows = pl.ds(b * W, W)
-        act_v[rows, pl.ds(0, C)] = jnp.where(col == 0, 0.0, pltpu.roll(v, 1, 0)).astype(BF16)
-        act_v[rows, pl.ds(C, C)] = v.astype(BF16)
-        act_v[rows, pl.ds(2 * C, C)] = jnp.where(col == W - 1, 0.0, pltpu.roll(v, W - 1, 0)).astype(
-            BF16
-        )
-
-    conv = dot(act_v[pl.ds(0, count)], wc_v[0])
-    conv = conv + dot(act_v[pl.ds(W, count)], wc_v[1])
-    conv = conv + dot(act_v[pl.ds(2 * W, count)], wc_v[2])
-    out[...] = (hid_v[...].astype(F32) + (conv + vec[4])).astype(BF16)
-
-    for t in range(parts):
-        for d in range(2):
-            ring_copy(d, own_piece(d, t), t).wait_send()
-
-    def drain(r, carry):
-        for d in range(2):
-            ref = piece(d, r, core)
-
-            @pl.when(r < steps - parts)
-            def _():
-                ring_copy(d, ref, r + parts).wait_send()
-
-            sib_copy(ref, d, r).wait_send()
-        return carry
-
-    lax.fori_loop(0, steps, drain, 0)
+        act_v[pl.ds(b * W, W)] = v.astype(BF16)
+
+    part = image_rows // 2
+
+    def convolve(h):
+        around = jnp.concatenate(
+            [act_v[pl.ds((h * part + i) * W, part * W)] for i in range(3)], axis=1
+        )
+        return {tap: dot(around, wc_v[tap].reshape(3 * C, C)) for tap in (0, 2, 1)}
+
+    def finish(h, taps):
+        for b in range(part):
+            rows = slice(b * W, (b + 1) * W)
+            left = jnp.where(col == 0, 0.0, pltpu.roll(taps[0][rows], 1, 0))
+            right = jnp.where(col == W - 1, 0.0, pltpu.roll(taps[2][rows], W - 1, 0))
+            conv = (left + right) + taps[1][rows]
+            here = pl.ds((h * part + b) * W, W)
+            out[here] = (hid_v[here].astype(F32) + (conv + vec[4])).astype(BF16)
+
+    for b in range(part + 2):
+        activate(b)
+    first = convolve(0)
+    for b in range(part + 2, image_rows + 2):
+        activate(b)
+    second = convolve(1)
+    finish(0, first)
+    finish(1, second)
+
     own_to_sib.wait_send()
     stats_all(st1, 0).wait_send()
     stats_all(st2, 1).wait_send()
@@ -391,6 +432,9 @@
     steps = (n // 4 - 1) * parts + parts // 2
     dma = pltpu.SemaphoreType.DMA
     vm = pltpu.VMEM
+    def stay(x):
+        return pltpu.with_memory_space_constraint(x, pltpu.HBM)
+
     result = pl.pallas_call(
         functools.partial(kernel, n),
         name="block",
@@ -404,17 +448,17 @@
             vm((C, C), BF16),
             vm((C, C), BF16),
             vm((C, C), BF16),
-            vm((3, 3 * C, C), BF16),
+            vm((3, 3, C, C), BF16),
             vm((count, C), BF16),
             vm((count, 128), F32),
             vm((count, 128), F32),
             vm((count, C), F32),
             vm((count, C), BF16),
             vm((2, W, C), BF16),
-            vm((count + 2 * W, 3 * C), BF16),
+            vm((count + 2 * W, C), BF16),
             vm((n, 2, 128), F32),
             vm((n, 2, 128), F32),
-            dma((12,)),
+            dma((15,)),
             dma((2, steps)),
             dma((2, steps)),
             dma((2, steps + 1)),
@@ -426,16 +470,16 @@
             dma((2,)),
         ],
         compiler_params=pltpu.CompilerParams(
-            collective_id=0, has_side_effects=True, vmem_limit_bytes=60 * 1024 * 1024
+            collective_id=0, has_side_effects=True, vmem_limit_bytes=40 * 1024 * 1024
         ),
     )(
-        latent.reshape(count, C),
-        *(v.reshape(1, C) for v in (g1, s1, g2, s2, bias)),
-        w_query,
-        w_key,
-        w_value,
-        w_out,
-        w_conv.reshape(3, 3 * C, C),
+        stay(latent.reshape(count, C)),
+        *(stay(v.reshape(1, C)) for v in (g1, s1, g2, s2, bias)),
+        stay(w_query),
+        stay(w_key),
+        stay(w_value),
+        stay(w_out),
+        stay(w_conv),
     )
     return result.reshape(rows, W, C)
 

time: 64 us -> 61.4 us (0.959)
  Pallas kernels: 62 us -> 60.5 us
  local copies, waits for them, and re-layouts: 1.87 us -> 0.8 us
    pallas_call x1, Pallas kernels: 62 us -> 60.5 us  [local(): pl.pallas_call(functools.partial(kernel, n), name='block', out_shape=jax....]
    unnamed x1, local copies, waits for them, and re-layouts: 1.87 us -> 0.8 us
where the time goes in v4:
time: 61.4 us; the launch traced here: 61.3 us
  Pallas kernels  60.5 us (99%)
  local copies, waits for them, and re-layouts  0.8 us (1%)
    pallas_call x1, Pallas kernels, local(): pl.pallas_call(functools.partial(kernel, n), name='block', out_shape=jax....  60.5 us

profile of v4, /device:TPU:1, one launch (start us, length us, event | category | flops | bytes accessed | tf_op | source)
XLA Modules:
  0.0 61.3 jit_solution(9330449801103535816)
XLA Ops:
  0.0 60.5 %block.1 = bf16[512,512]{1,0:T(8,128)(2,1)S(1)} custom-call(bf16[512,512]{1,0:T(8,128)(2,1)} %bitcast.8, f32[1,512]{1,0:T(1,128)} %bitcast.9, f32[1,512]{1,0:T(1,128)} %bitcast.10, f32[1,512]{1,0:T(1,128)} %bitcast.11, f32[1,512]{1,0:T(1,128)} %bitcast.12, f32[1,512]{1,0:T(1,128)} %bitcast.13, bf16[512,512]{1,0:T(8,128)(2,1)} %wq.1, bf16[512,512]{1,0:T(8,128)(2,1)} %wk.1, ...), custom_call_target="tpu_custom_call" | custom-call | tf_op jit(solution)/shard_map/block/pallas_call | solution.py:438
  60.5 0.8 %copy.13 = bf16[4,128,512]{2,1,0:T(8,128)(2,1)} copy(bf16[4,128,512]{2,1,0:T(8,128)(2,1)S(1)} %bitcast.7) | data formatting | bytes 1048576

commit v5 on v4

--- a/solution.py
+++ b/solution.py
@@ -12,7 +12,8 @@
 GROUP = 16
 W = 128
 EPS = 1e-06
-PIECE = 128
+PIECE = 256
+LAST = (128, 64, 64)
 LOG2E = 1.4426950408889634
 F32 = jnp.float32
 BF16 = jnp.bfloat16
@@ -81,9 +82,9 @@
     second = jnp.sum(seconds + size * (off * off), axis=0, keepdims=True)
     scale = lax.rsqrt(second * (1.0 / (devices * size)) + EPS)
     at = lax.broadcasted_iota(jnp.int32, (8, 128), 0)
-    lane = lax.broadcasted_iota(jnp.int32, (8, 128), 1) % GROUP
+    lane = lax.broadcasted_iota(jnp.int32, (8, 128), 1)
     both = jnp.where(at < C // 128, centre, scale)
-    both = group_total(jnp.where(lane == at % (C // 128), both, 0.0))
+    both = jnp.take_along_axis(both, lane // GROUP * GROUP + at % (C // 128), axis=1)
     centre, scale = (
         jnp.concatenate([both[k : k + 1] for k in range(first, first + C // 128)], axis=1)
         for first in (0, C // 128)
@@ -148,7 +149,9 @@
     count = lat.shape[0]
     parts = count // PIECE
     half = chips // 2
-    steps = (half - 1) * parts + parts // 2
+    steps = (half - 1) * parts
+    ends = len(LAST)
+    assert parts == 2 and sum(LAST) == PIECE
     nexts = (
         lax.rem(z + 1, chips) * 2 + core,
         lax.rem(z + chips - 1, chips) * 2 + core,
@@ -175,6 +178,16 @@
         slot, at = place(d, r, c)
         return gathered.at[slot, pl.ds(pl.multiple_of(at, PIECE), PIECE)]
 
+    def last(d, k, c):
+        at = (PIECE if d else 0) + sum(LAST[:k])
+        return gathered.at[lax.rem(z + half, chips) * 2 + c, pl.ds(at, LAST[k])]
+
+    def last_on(d, k):
+        at = (PIECE if d else 0) + sum(LAST[:k])
+        hop = half - 1
+        chip = lax.rem(z + chips - hop, chips) if d == 0 else lax.rem(z + hop, chips)
+        return gathered.at[chip * 2 + core, pl.ds(at, LAST[k])]
+
     def ring_copy(d, ref, t):
         return pltpu.make_async_remote_copy(
             src_ref=ref,
@@ -203,7 +216,7 @@
     for t in range(parts):
         for d in range(2):
             ring_copy(d, own_piece(d, t), t).start()
-    own_to_sib = sib_copy(gathered.at[me], 0, steps)
+    own_to_sib = sib_copy(gathered.at[me], 0, steps + ends)
     own_to_sib.start()
     greet(heard.at[0])
     gets = []
@@ -233,6 +246,37 @@
             device_id_type=MESH,
         )
 
+    def alike_copy(k):
+        return pltpu.make_async_remote_copy(
+            src_ref=st1.at[0],
+            dst_ref=st1.at[k // 2],
+            send_sem=st_send.at[0],
+            recv_sem=st_recv.at[0],
+            device_id={"row": lax.rem(me + k, n)},
+            device_id_type=MESH,
+        )
+
+    def alike_all():
+        some = st1.at[pl.ds(1, chips - 1)]
+        return pltpu.make_async_remote_copy(
+            src_ref=some,
+            dst_ref=some,
+            send_sem=st_send.at[0],
+            recv_sem=st_recv.at[0],
+            device_id={"row": sib},
+            device_id_type=MESH,
+        )
+
+    def alike_over():
+        return pltpu.make_async_remote_copy(
+            src_ref=st1.at[pl.ds(0, chips)],
+            dst_ref=st1.at[pl.ds(chips, chips)],
+            send_sem=st_send.at[2],
+            recv_sem=st_recv.at[2],
+            device_id={"row": sib},
+            device_id_type=MESH,
+        )
+
     def stats_all(buf, which):
         return pltpu.make_async_remote_copy(
             src_ref=buf.at[pl.ds(1, n - 1)],
@@ -253,7 +297,8 @@
         if k + 1 < rounds:
             greet(heard.at[k + 1])
     for k in farthest:
-        stats_copy(st1, 0, k).start()
+        if k % 2 == 0:
+            alike_copy(k).start()
 
     gets[2].wait()
     gets[3].wait()
@@ -268,11 +313,24 @@
             def _():
                 ring_copy(d, ref, r + parts).start()
 
+            @pl.when(r == steps - parts)
+            def _():
+                for k in range(ends):
+                    ring_copy(d, last_on(d, k), steps + k).start()
+
             sib_copy(ref, d, r).start()
 
-    for r in range(parts):
-        comm(r)
-    stats_all(st1, 0).wait_recv()
+    def comm_last(k):
+        for d in range(2):
+            ref = last(d, k, core)
+            ring_copy(d, ref, steps + k).wait_recv()
+            sib_copy(ref, d, steps + k).start()
+
+    comm(0)
+    alike_all().wait_recv()
+    alike_over().start()
+    comm(1)
+    alike_over().wait_recv()
     for g in get_vecs:
         g.wait()
     a1, b1, centre1 = affine(st1[:, 0], st1[:, 1], float(count), vec[0], vec[1])
@@ -312,7 +370,7 @@
         attend(jnp.concatenate(pieces(r, core) + pieces(r, 1 - core), axis=0))
 
     attend(gathered[me])
-    sib_copy(gathered.at[sib], 0, steps).wait_recv()
+    sib_copy(gathered.at[sib], 0, steps + ends).wait_recv()
     attend(gathered[sib])
     lax.fori_loop(0, parts - 1, lambda r, carry: (compute(r), carry)[1], 0)
 
@@ -322,10 +380,24 @@
         return carry
 
     lax.fori_loop(parts, steps, step, 0)
-    attend(jnp.concatenate(pieces(steps - 1, core), axis=0))
-    for d in range(2):
-        sib_copy(piece(d, steps - 1, 1 - core), d, steps - 1).wait_recv()
-    attend(jnp.concatenate(pieces(steps - 1, 1 - core), axis=0))
+    compute(steps - 1)
+
+    def lasts(k, c):
+        return [last(d, k, c)[...] for d in range(2)]
+
+    def wait_last(k):
+        for d in range(2):
+            sib_copy(last(d, k, 1 - core), d, steps + k).wait_recv()
+
+    comm_last(0)
+    comm_last(1)
+    wait_last(0)
+    attend(jnp.concatenate(lasts(0, core) + lasts(0, 1 - core), axis=0))
+    comm_last(2)
+    wait_last(1)
+    attend(jnp.concatenate(lasts(1, core) + lasts(1, 1 - core) + lasts(2, core), axis=0))
+    wait_last(2)
+    attend(jnp.concatenate(lasts(2, 1 - core), axis=0))
 
     total = jnp.sum(l_v[...], axis=1, keepdims=True)
     attended = (acc_v[...] * (1.0 / total) * a1 + b1).astype(BF16)
@@ -367,6 +439,10 @@
         return carry
 
     lax.fori_loop(0, steps, drain, 0)
+    for k in range(ends):
+        for d in range(2):
+            ring_copy(d, last_on(d, k), steps + k).wait_send()
+            sib_copy(last(d, k, core), d, steps + k).wait_send()
     for g in get_taps:
         g.wait()
     stats_all(st2, 1).wait_recv()
@@ -419,7 +495,8 @@
     finish(1, second)
 
     own_to_sib.wait_send()
-    stats_all(st1, 0).wait_send()
+    alike_all().wait_send()
+    alike_over().wait_send()
     stats_all(st2, 1).wait_send()
     for i in range(2):
         halo_copy(i).wait_send()
@@ -429,7 +506,7 @@
     rows = latent.shape[0]
     count = rows * W
     parts = count // PIECE
-    steps = (n // 4 - 1) * parts + parts // 2
+    steps = (n // 4 - 1) * parts + len(LAST)
     dma = pltpu.SemaphoreType.DMA
     vm = pltpu.VMEM
     def stay(x):
@@ -464,8 +541,8 @@
             dma((2, steps + 1)),
             dma((2, steps + 1)),
             pltpu.SemaphoreType.REGULAR((n // 4 - 1,)),
-            dma((2,)),
-            dma((2,)),
+            dma((3,)),
+            dma((3,)),
             dma((2,)),
             dma((2,)),
         ],

time: 61.4 us -> 60.5 us (0.985)
  Pallas kernels: 60.5 us -> 59.5 us
    pallas_call x1, Pallas kernels: 60.5 us -> 59.5 us  [local(): pl.pallas_call(functools.partial(kernel, n), name='block', out_shape=jax....]
where the time goes in v5:
time: 60.5 us; the launch traced here: 60.3 us
  Pallas kernels  59.5 us (98%)
  local copies, waits for them, and re-layouts  0.8 us (1%)
    pallas_call x1, Pallas kernels, local(): pl.pallas_call(functools.partial(kernel, n), name='block', out_shape=jax....  59.5 us

profile of v5, /device:TPU:1, one launch (start us, length us, event | category | flops | bytes accessed | tf_op | source)
XLA Modules:
  0.0 60.3 jit_solution(18253117562978933813)
XLA Ops:
  0.0 59.5 %block.1 = bf16[512,512]{1,0:T(8,128)(2,1)S(1)} custom-call(bf16[512,512]{1,0:T(8,128)(2,1)} %bitcast.8, f32[1,512]{1,0:T(1,128)} %bitcast.9, f32[1,512]{1,0:T(1,128)} %bitcast.10, f32[1,512]{1,0:T(1,128)} %bitcast.11, f32[1,512]{1,0:T(1,128)} %bitcast.12, f32[1,512]{1,0:T(1,128)} %bitcast.13, bf16[512,512]{1,0:T(8,128)(2,1)} %wq.1, bf16[512,512]{1,0:T(8,128)(2,1)} %wk.1, ...), custom_call_target="tpu_custom_call" | custom-call | tf_op jit(solution)/shard_map/block/pallas_call | solution.py:515
  59.6 0.8 %copy.13 = bf16[4,128,512]{2,1,0:T(8,128)(2,1)} copy(bf16[4,128,512]{2,1,0:T(8,128)(2,1)S(1)} %bitcast.7) | data formatting | bytes 1048576

commit v6 on v5

--- a/solution.py
+++ b/solution.py
@@ -122,6 +122,7 @@
     wv_v,
     wo_v,
     wc_v,
+    wd_v,
     q_v,
     m_v,
     l_v,
@@ -372,6 +373,14 @@
     attend(gathered[me])
     sib_copy(gathered.at[sib], 0, steps + ends).wait_recv()
     attend(gathered[sib])
+
+    for g in get_taps:
+        g.wait()
+    for tap in range(3):
+        ends_of = wc_v[tap, 0].astype(F32) + wc_v[tap, 2].astype(F32)
+        middle = wc_v[tap, 1].astype(F32)
+        wc_v[tap, 1] = ((ends_of + middle) * 0.5).astype(BF16)
+        wd_v[tap] = ((ends_of - middle) * 0.5).astype(BF16)
     lax.fori_loop(0, parts - 1, lambda r, carry: (compute(r), carry)[1], 0)
 
     def step(r, carry):
@@ -443,8 +452,6 @@
         for d in range(2):
             ring_copy(d, last_on(d, k), steps + k).wait_send()
             sib_copy(last(d, k, core), d, steps + k).wait_send()
-    for g in get_taps:
-        g.wait()
     stats_all(st2, 1).wait_recv()
     a2, b2, _ = affine(st2[:, 0], st2[:, 1], float(count), vec[2], vec[3])
     for i in range(2):
@@ -468,31 +475,36 @@
             v = jnp.where(me < n - 1, v, 0.0)
         act_v[pl.ds(b * W, W)] = v.astype(BF16)
 
-    part = image_rows // 2
-
-    def convolve(h):
-        around = jnp.concatenate(
-            [act_v[pl.ds((h * part + i) * W, part * W)] for i in range(3)], axis=1
-        )
-        return {tap: dot(around, wc_v[tap].reshape(3 * C, C)) for tap in (0, 2, 1)}
-
-    def finish(h, taps):
-        for b in range(part):
-            rows = slice(b * W, (b + 1) * W)
-            left = jnp.where(col == 0, 0.0, pltpu.roll(taps[0][rows], 1, 0))
-            right = jnp.where(col == W - 1, 0.0, pltpu.roll(taps[2][rows], W - 1, 0))
-            conv = (left + right) + taps[1][rows]
-            here = pl.ds((h * part + b) * W, W)
-            out[here] = (hid_v[here].astype(F32) + (conv + vec[4])).astype(BF16)
-
-    for b in range(part + 2):
+    for b in range(image_rows + 2):
         activate(b)
-    first = convolve(0)
-    for b in range(part + 2, image_rows + 2):
-        activate(b)
-    second = convolve(1)
-    finish(0, first)
-    finish(1, second)
+
+    def row(b):
+        return act_v[pl.ds(b * W, W)].astype(F32)
+
+    pairs = range(0, image_rows, 2)
+
+    def product(make, weights):
+        left = jnp.concatenate([make(b).astype(BF16) for b in pairs], axis=0)
+        return dot(left, jnp.concatenate(weights, axis=1))
+
+    p1 = product(lambda b: row(b + 1) + row(b + 2), [wc_v[tap, 1] for tap in range(3)])
+    p2 = product(lambda b: row(b + 2) - row(b + 1), [wd_v[tap] for tap in range(3)])
+    p0 = product(lambda b: row(b) - row(b + 2), [wc_v[tap, 0] for tap in range(3)])
+    p3 = product(lambda b: row(b + 1) - row(b + 3), [wc_v[tap, 2] for tap in range(3)])
+
+    def finish(b, taps):
+        left = jnp.where(col == 0, 0.0, pltpu.roll(taps[:, :C], 1, 0))
+        right = jnp.where(col == W - 1, 0.0, pltpu.roll(taps[:, 2 * C :], W - 1, 0))
+        conv = (left + right) + taps[:, C : 2 * C]
+        here = pl.ds(b * W, W)
+        out[here] = (hid_v[here].astype(F32) + (conv + vec[4])).astype(BF16)
+
+    for k, b in enumerate(pairs):
+        rows = slice(k * W, (k + 1) * W)
+        finish(b, p1[rows] + p2[rows] + p0[rows])
+    for k, b in enumerate(pairs):
+        rows = slice(k * W, (k + 1) * W)
+        finish(b + 1, p1[rows] - p2[rows] - p3[rows])
 
     own_to_sib.wait_send()
     alike_all().wait_send()
@@ -526,6 +538,7 @@
             vm((C, C), BF16),
             vm((C, C), BF16),
             vm((3, 3, C, C), BF16),
+            vm((3, C, C), BF16),
             vm((count, C), BF16),
             vm((count, 128), F32),
             vm((count, 128), F32),

time: 60.5 us -> 60 us (level)
  no operation moved by 1% of the time
where the time goes in v6:
time: 60 us; the launch traced here: 59.8 us
  Pallas kernels  59 us (98%)
  local copies, waits for them, and re-layouts  0.8 us (1%)
    pallas_call x1, Pallas kernels, local(): pl.pallas_call(functools.partial(kernel, n), name='block', out_shape=jax....  59 us

profile of v6, /device:TPU:1, one launch (start us, length us, event | category | flops | bytes accessed | tf_op | source)
XLA Modules:
  0.0 59.8 jit_solution(8473476299624850691)
XLA Ops:
  0.0 59.0 %block.1 = bf16[512,512]{1,0:T(8,128)(2,1)S(1)} custom-call(bf16[512,512]{1,0:T(8,128)(2,1)} %bitcast.8, f32[1,512]{1,0:T(1,128)} %bitcast.9, f32[1,512]{1,0:T(1,128)} %bitcast.10, f32[1,512]{1,0:T(1,128)} %bitcast.11, f32[1,512]{1,0:T(1,128)} %bitcast.12, f32[1,512]{1,0:T(1,128)} %bitcast.13, bf16[512,512]{1,0:T(8,128)(2,1)} %wq.1, bf16[512,512]{1,0:T(8,128)(2,1)} %wk.1, ...), custom_call_target="tpu_custom_call" | custom-call | tf_op jit(solution)/shard_map/block/pallas_call | solution.py:527
  59.0 0.8 %copy.13 = bf16[4,128,512]{2,1,0:T(8,128)(2,1)} copy(bf16[4,128,512]{2,1,0:T(8,128)(2,1)S(1)} %bitcast.7) | data formatting | bytes 1048576

commit v7 on v6

--- a/solution.py
+++ b/solution.py
@@ -454,8 +454,6 @@
             sib_copy(last(d, k, core), d, steps + k).wait_send()
     stats_all(st2, 1).wait_recv()
     a2, b2, _ = affine(st2[:, 0], st2[:, 1], float(count), vec[2], vec[3])
-    for i in range(2):
-        halo_copy(i).wait_recv()
 
     col = lax.broadcasted_iota(jnp.int32, (W, C), 0)
     image_rows = count // W
@@ -475,7 +473,7 @@
             v = jnp.where(me < n - 1, v, 0.0)
         act_v[pl.ds(b * W, W)] = v.astype(BF16)
 
-    for b in range(image_rows + 2):
+    for b in range(1, image_rows + 1):
         activate(b)
 
     def row(b):
@@ -489,6 +487,10 @@
 
     p1 = product(lambda b: row(b + 1) + row(b + 2), [wc_v[tap, 1] for tap in range(3)])
     p2 = product(lambda b: row(b + 2) - row(b + 1), [wd_v[tap] for tap in range(3)])
+    for i in range(2):
+        halo_copy(i).wait_recv()
+    activate(0)
+    activate(image_rows + 1)
     p0 = product(lambda b: row(b) - row(b + 2), [wc_v[tap, 0] for tap in range(3)])
     p3 = product(lambda b: row(b + 1) - row(b + 3), [wc_v[tap, 2] for tap in range(3)])
 

time: 60 us -> 60.3 us (level)
  no operation moved by 1% of the time
where the time goes in v7:
time: 60.3 us; the launch traced here: 60.2 us
  Pallas kernels  59.4 us (99%)
  local copies, waits for them, and re-layouts  0.8 us (1%)
    pallas_call x1, Pallas kernels, local(): pl.pallas_call(functools.partial(kernel, n), name='block', out_shape=jax....  59.4 us

profile of v7, /device:TPU:1, one launch (start us, length us, event | category | flops | bytes accessed | tf_op | source)
XLA Modules:
  0.0 60.2 jit_solution(17415086958626971530)
XLA Ops:
  0.0 59.4 %block.1 = bf16[512,512]{1,0:T(8,128)(2,1)S(1)} custom-call(bf16[512,512]{1,0:T(8,128)(2,1)} %bitcast.8, f32[1,512]{1,0:T(1,128)} %bitcast.9, f32[1,512]{1,0:T(1,128)} %bitcast.10, f32[1,512]{1,0:T(1,128)} %bitcast.11, f32[1,512]{1,0:T(1,128)} %bitcast.12, f32[1,512]{1,0:T(1,128)} %bitcast.13, bf16[512,512]{1,0:T(8,128)(2,1)} %wq.1, bf16[512,512]{1,0:T(8,128)(2,1)} %wk.1, ...), custom_call_target="tpu_custom_call" | custom-call | tf_op jit(solution)/shard_map/block/pallas_call | solution.py:529
  59.4 0.8 %copy.13 = bf16[4,128,512]{2,1,0:T(8,128)(2,1)} copy(bf16[4,128,512]{2,1,0:T(8,128)(2,1)S(1)} %bitcast.7) | data formatting | bytes 1048576
